TPU v7x, 32 devices: a 4x4x1 block of a 4x4x8 slice. The times are simulated.
32 devices in a mesh: dp: 1 (over z), tp: 4 (over y), cp: 8 (over x, core).
Axes of the slice: x: 4, y: 4, z: 1, core: 2. Of those that a mesh axis runs over, the one named last changes fastest.
The devices are a block of a 4x4x8 slice.
Arguments:
- x: bfloat16 [2048, 5120], P(('dp', 'cp'))
- k_cache: bfloat16 [32768, 8, 128], P(('dp', 'cp'), 'tp')
- v_cache: bfloat16 [32768, 8, 128], P(('dp', 'cp'), 'tp')
- rope_table: float32 [2048, 64], P(('dp', 'cp'))
- norm_gain: bfloat16 [5120], replicated
- w_qkv: bfloat16 [5120, 14336], P(None, 'tp')
- b_qkv: bfloat16 [14336], P('tp')
- w_out: bfloat16 [12288, 5120], P('tp')
Outputs:
- output 1: bfloat16 [2048, 5120], P(('dp', 'cp'))
- output 2: bfloat16 [2048, 8, 128], P(('dp', 'cp'), 'tp')
- output 3: bfloat16 [2048, 8, 128], P(('dp', 'cp'), 'tp')
All inputs are finite; a program needn't handle non-finite values.
Results may differ from a plain program's by a relative error of at most 0.00328593.
Values are sent between devices in bfloat16 or wider.
A program may use at most 768 MiB of HBM per device.

v0:
```python
import jax
import jax.numpy as jnp
from jax import lax
from jax.sharding import PartitionSpec as P, NamedSharding

EPS = 1.5625e-07
MASK_VALUE = -1e30


def apply_rotary(vals, cos_t, sin_t):
    pair_count = cos_t.shape[-1]
    lead_shape = vals.shape[:-1]
    paired = vals[..., :2 * pair_count].reshape(lead_shape + (pair_count, 2))
    even_part = paired[..., 0]
    odd_part = paired[..., 1]
    turned = jnp.stack([even_part * cos_t - odd_part * sin_t, odd_part * cos_t + even_part * sin_t], axis=-1)
    return jnp.concatenate([turned.reshape(lead_shape + (2 * pair_count,)), vals[..., 2 * pair_count:]], axis=-1)


def project_new(x, rope_table, norm_gain, w_qkv, b_qkv, kv_count, head_dim):
    x_f32 = x.astype(jnp.float32)
    inv_rms = lax.rsqrt(jnp.mean(x_f32 * x_f32, axis=-1, keepdims=True) + EPS)
    hidden = (x_f32 * inv_rms * norm_gain.astype(jnp.float32)).astype(jnp.bfloat16)
    tok_rows = x.shape[0]
    group = w_qkv.shape[1] // (kv_count * head_dim) - 2
    qkv_all = jnp.dot(hidden, w_qkv, preferred_element_type=jnp.float32) + b_qkv.astype(jnp.float32)
    qkv_all = qkv_all.reshape(tok_rows, kv_count, group + 2, head_dim)
    pair_count = rope_table.shape[1] // 2
    cos_t = rope_table[:, :pair_count]
    sin_t = rope_table[:, pair_count:]
    queries = apply_rotary(qkv_all[:, :, :group], cos_t[:, None, None], sin_t[:, None, None]).astype(jnp.bfloat16)
    new_k = apply_rotary(qkv_all[:, :, group], cos_t[:, None], sin_t[:, None]).astype(jnp.bfloat16)
    new_v = qkv_all[:, :, group + 1].astype(jnp.bfloat16)
    return x_f32, queries, new_k, new_v


def local_step(x, k_cache, v_cache, rope_table, norm_gain, w_qkv, b_qkv, w_out):
    kv_local, head_dim = k_cache.shape[1], k_cache.shape[2]
    tok_rows = x.shape[0]
    x_f32, queries, new_k, new_v = project_new(x, rope_table, norm_gain, w_qkv, b_qkv, kv_local, head_dim)
    group = queries.shape[2]
    k_prefix = lax.all_gather(k_cache, 'cp')
    v_prefix = lax.all_gather(v_cache, 'cp')
    k_recent = lax.all_gather(new_k, 'cp')
    v_recent = lax.all_gather(new_v, 'cp')
    cp_size = k_prefix.shape[0]
    scale = head_dim ** -0.5
    q_pos = lax.axis_index('cp') * tok_rows + jnp.arange(tok_rows)

    def attend(carry, block):
        run_max, run_sum, weighted = carry
        kp_block, vp_block, kr_block, vr_block, source = block
        s_pref = jnp.einsum('tngd,knd->tngk', queries, kp_block, preferred_element_type=jnp.float32) * scale
        s_recent = jnp.einsum('tngd,knd->tngk', queries, kr_block, preferred_element_type=jnp.float32) * scale
        k_pos = source * tok_rows + jnp.arange(tok_rows)
        visible = (k_pos[None, :] <= q_pos[:, None])[:, None, None, :]
        s_recent = jnp.where(visible, s_recent, MASK_VALUE)
        new_max = jnp.maximum(run_max, jnp.maximum(s_pref.max(axis=-1), s_recent.max(axis=-1)))
        rescale = jnp.exp(run_max - new_max)
        p_pref = jnp.exp(s_pref - new_max[..., None])
        p_recent = jnp.exp(s_recent - new_max[..., None])
        run_sum = run_sum * rescale + p_pref.sum(axis=-1) + p_recent.sum(axis=-1)
        weighted = (weighted * rescale[..., None]
                    + jnp.einsum('tngk,knd->tngd', p_pref.astype(jnp.bfloat16), vp_block, preferred_element_type=jnp.float32)
                    + jnp.einsum('tngk,knd->tngd', p_recent.astype(jnp.bfloat16), vr_block, preferred_element_type=jnp.float32))
        return (new_max, run_sum, weighted), None

    stat_shape = (tok_rows, kv_local, group)
    start_carry = (jnp.full(stat_shape, MASK_VALUE, jnp.float32), jnp.zeros(stat_shape, jnp.float32), jnp.zeros(stat_shape + (head_dim,), jnp.float32))
    (run_max, run_sum, weighted), _ = lax.scan(attend, start_carry, (k_prefix, v_prefix, k_recent, v_recent, jnp.arange(cp_size)))
    attn = (weighted / run_sum[..., None]).astype(jnp.bfloat16).reshape(tok_rows, kv_local * group * head_dim)
    proj_part = jnp.dot(attn, w_out, preferred_element_type=jnp.float32)
    y = (x_f32 + lax.psum(proj_part, 'tp')).astype(jnp.bfloat16)
    return y, new_k, new_v


def solution(mesh):
    row_spec = P(('dp', 'cp'), None)
    cache_spec = P(('dp', 'cp'), 'tp', None)
    return jax.shard_map(local_step, mesh=mesh, in_specs=(row_spec, cache_spec, cache_spec, row_spec, P(None), P(None, 'tp'), P('tp'), P('tp', None)), out_specs=(row_spec, cache_spec, cache_spec), check_vma=False)
```

profile of v0, /device:TPU:97, one launch (start us, length us, event | category | flops | bytes accessed | tf_op | source)
XLA Modules:
  0.0 1327.0 jit_solution(8885317765192683579)
XLA Ops:
  7.2 2.3 fusion.39
  11.0 18.4 %convolution_add_fusion = f32[256,3584]{1,0:T(8,128)} fusion(bf16[5120,3584]{1,0:T(8,128)(2,1)} %param.15, bf16[256,5120]{1,0:T(8,128)(2,1)} %param.10, f32[5120]{0:T(1024)S(1)} %convert_element_type.50, f32[256]{0:T(256)S(1)} %add_rsqrt_fusion, f32[3584]{0:T(1024)S(1)} %convert_element_type.52), kind=kOutput, calls=%fused_computation.48 | convolution fusion | flops 9401401344 | bytes 43027456 | tf_op jit(solution)/shard_map/dot_general | solution.py:26
  29.4 5.3 copy.44
  34.7 1.6 slice.75
  39.3 1.6 copy.43
  41.0 3.2 copy.50
  50.8 1.6 copy.52
  52.4 9.0 all-gather.14.cloned.1.call-done
  64.1 20.9 %all-gather.8.cloned.1.call-done = bf16[8,256,2,128]{3,1,2,0:T(8,128)(2,1)} async-done(((bf16[1,256,2,128]{3,1,2,0:T(8,128)(2,1)}), bf16[8,256,2,128]{3,1,2,0:T(8,128)(2,1)}) %all-gather.8.cloned.1.call-update) | async-done | bytes 1048592 | tf_op jit(solution)/shard_map/all_gather | solution.py:44
  85.1 84.7 %all-gather.10.cloned.1.call-done = bf16[32768,2,128]{2,0,1:T(8,128)(2,1)} async-done(((bf16[4096,2,128]{2,0,1:T(8,128)(2,1)}), bf16[32768,2,128]{2,0,1:T(8,128)(2,1)}) %all-gather.10.cloned.1.call-update) | async-done | bytes 16777232 | tf_op jit(solution)/shard_map/all_gather | solution.py:42
  169.8 84.6 %all-gather.12.cloned.1.call-done = bf16[32768,2,128]{2,0,1:T(8,128)(2,1)} async-done(((bf16[4096,2,128]{2,0,1:T(8,128)(2,1)}), bf16[32768,2,128]{2,0,1:T(8,128)(2,1)}) %all-gather.12.cloned.1.call-update) | async-done | bytes 16777232 | tf_op jit(solution)/shard_map/all_gather | solution.py:43
  254.4 938.0 %while.15 = (s32[]{:T(128)}, f32[256,2,12]{0,2,1:T(8,128)S(1)}, f32[256,2,12]{0,2,1:T(8,128)S(1)}, f32[256,2,12,128]{0,3,2,1:T(8,128)}, bf16[8,4096,2,128]{3,1,0...) while((s32[]{:T(128)}, f32[256,2,12]{0,2,1:T(8,128)S(1)}, ...), condition=%wide.region_6.7_spmd.clone, body=%wide.region_1.6_spmd.clone.sunk | while | flops 13912078336 | bytes 367022272 | solution.py:70
  255.8 5.2 fusion.70
  260.9 36.4 %bitcast_reduce_fusion.2 = (f32[256,2,12]{0,2,1:T(8,128)S(1)}, f32[2,4096,256,12]{2,1,3,0:T(8,128)}) fusion(bf16[256,2,12,128]{3,0,2,1:T(8,128)(2,1)} %get-tuple-element.293, bf16[8,4096,2,128]{3,1,0,2:T(8,128)(2,1)} %get-tuple-element.292, s32[]{:T(128)S(6)} %copy.71), kind=kOutput, calls=%fused_computation.2.clone.1 | convolution fusion | flops 6492776448 | bytes 104357888 | tf_op jit(solution)/shard_map/while/body/eval_jaxpr/tngd,knd->tngk/dot_general | solution.py:53
  297.4 31.1 %fusion.72 = f32[256,2,12]{0,2,1:T(8,128)S(1)} fusion(f32[2,4096,256,12]{2,1,3,0:T(8,128)} %get-tuple-element.257, f32[256,2,12]{0,2,1:T(8,128)S(1)} %maximum_maximum_fusion.2), kind=kLoop, calls=%fused_computation.5.clone.1 | loop fusion | flops 75491328 | bytes 100712448 | tf_op jit(solution)/shard_map/while/body/eval_jaxpr/reduce_sum | solution.py:62
  328.5 4.3 fusion.71
  333.1 2.6 fusion.74
  335.7 35.3 %bitcast_add_fusion.3 = f32[256,2,12,128]{0,3,2,1:T(8,128)} fusion(f32[2,128,256,12]{2,1,3,0:T(8,128)S(1)} %fusion.74, f32[256,2,12,128]{0,3,2,1:T(8,128)} %get-tuple-element.277, f32[2,4096,256,12]{2,1,3,0:T(8,128)} %get-tuple-element.257, f32[256,2,12]{0,2,1:T(8,128)S(1)} %maximum_maximum_fusion.2, ...), kind=kOutput, calls=%fused_computation.13.clone.1 | convolution fusion | flops 6521094144 | bytes 112246792 | tf_op jit(solution)/shard_map/while/body/eval_jaxpr/tngk,knd->tngd/dot_general | solution.py:64
  372.3 5.2 fusion.70
  377.5 36.4 %bitcast_reduce_fusion.2 = (f32[256,2,12]{0,2,1:T(8,128)S(1)}, f32[2,4096,256,12]{2,1,3,0:T(8,128)}) fusion(bf16[256,2,12,128]{3,0,2,1:T(8,128)(2,1)} %get-tuple-element.293, bf16[8,4096,2,128]{3,1,0,2:T(8,128)(2,1)} %get-tuple-element.292, s32[]{:T(128)S(6)} %copy.71), kind=kOutput, calls=%fused_computation.2.clone.1 | convolution fusion | flops 6492776448 | bytes 104357888 | tf_op jit(solution)/shard_map/while/body/eval_jaxpr/tngd,knd->tngk/dot_general | solution.py:53
  413.9 31.1 %fusion.72 = f32[256,2,12]{0,2,1:T(8,128)S(1)} fusion(f32[2,4096,256,12]{2,1,3,0:T(8,128)} %get-tuple-element.257, f32[256,2,12]{0,2,1:T(8,128)S(1)} %maximum_maximum_fusion.2), kind=kLoop, calls=%fused_computation.5.clone.1 | loop fusion | flops 75491328 | bytes 100712448 | tf_op jit(solution)/shard_map/while/body/eval_jaxpr/reduce_sum | solution.py:62
  445.0 4.3 fusion.71
  449.6 2.6 fusion.74
  452.3 36.1 %bitcast_add_fusion.3 = f32[256,2,12,128]{0,3,2,1:T(8,128)} fusion(f32[2,128,256,12]{2,1,3,0:T(8,128)S(1)} %fusion.74, f32[256,2,12,128]{0,3,2,1:T(8,128)} %get-tuple-element.277, f32[2,4096,256,12]{2,1,3,0:T(8,128)} %get-tuple-element.257, f32[256,2,12]{0,2,1:T(8,128)S(1)} %maximum_maximum_fusion.2, ...), kind=kOutput, calls=%fused_computation.13.clone.1 | convolution fusion | flops 6521094144 | bytes 112246792 | tf_op jit(solution)/shard_map/while/body/eval_jaxpr/tngk,knd->tngd/dot_general | solution.py:64
  489.7 5.2 fusion.70
  494.9 36.4 %bitcast_reduce_fusion.2 = (f32[256,2,12]{0,2,1:T(8,128)S(1)}, f32[2,4096,256,12]{2,1,3,0:T(8,128)}) fusion(bf16[256,2,12,128]{3,0,2,1:T(8,128)(2,1)} %get-tuple-element.293, bf16[8,4096,2,128]{3,1,0,2:T(8,128)(2,1)} %get-tuple-element.292, s32[]{:T(128)S(6)} %copy.71), kind=kOutput, calls=%fused_computation.2.clone.1 | convolution fusion | flops 6492776448 | bytes 104357888 | tf_op jit(solution)/shard_map/while/body/eval_jaxpr/tngd,knd->tngk/dot_general | solution.py:53
  531.3 31.1 %fusion.72 = f32[256,2,12]{0,2,1:T(8,128)S(1)} fusion(f32[2,4096,256,12]{2,1,3,0:T(8,128)} %get-tuple-element.257, f32[256,2,12]{0,2,1:T(8,128)S(1)} %maximum_maximum_fusion.2), kind=kLoop, calls=%fused_computation.5.clone.1 | loop fusion | flops 75491328 | bytes 100712448 | tf_op jit(solution)/shard_map/while/body/eval_jaxpr/reduce_sum | solution.py:62
  562.4 4.3 fusion.71
  567.0 2.6 fusion.74
  569.6 36.1 %bitcast_add_fusion.3 = f32[256,2,12,128]{0,3,2,1:T(8,128)} fusion(f32[2,128,256,12]{2,1,3,0:T(8,128)S(1)} %fusion.74, f32[256,2,12,128]{0,3,2,1:T(8,128)} %get-tuple-element.277, f32[2,4096,256,12]{2,1,3,0:T(8,128)} %get-tuple-element.257, f32[256,2,12]{0,2,1:T(8,128)S(1)} %maximum_maximum_fusion.2, ...), kind=kOutput, calls=%fused_computation.13.clone.1 | convolution fusion | flops 6521094144 | bytes 112246792 | tf_op jit(solution)/shard_map/while/body/eval_jaxpr/tngk,knd->tngd/dot_general | solution.py:64
  607.0 5.2 fusion.70
  612.2 36.4 %bitcast_reduce_fusion.2 = (f32[256,2,12]{0,2,1:T(8,128)S(1)}, f32[2,4096,256,12]{2,1,3,0:T(8,128)}) fusion(bf16[256,2,12,128]{3,0,2,1:T(8,128)(2,1)} %get-tuple-element.293, bf16[8,4096,2,128]{3,1,0,2:T(8,128)(2,1)} %get-tuple-element.292, s32[]{:T(128)S(6)} %copy.71), kind=kOutput, calls=%fused_computation.2.clone.1 | convolution fusion | flops 6492776448 | bytes 104357888 | tf_op jit(solution)/shard_map/while/body/eval_jaxpr/tngd,knd->tngk/dot_general | solution.py:53
  648.6 31.1 %fusion.72 = f32[256,2,12]{0,2,1:T(8,128)S(1)} fusion(f32[2,4096,256,12]{2,1,3,0:T(8,128)} %get-tuple-element.257, f32[256,2,12]{0,2,1:T(8,128)S(1)} %maximum_maximum_fusion.2), kind=kLoop, calls=%fused_computation.5.clone.1 | loop fusion | flops 75491328 | bytes 100712448 | tf_op jit(solution)/shard_map/while/body/eval_jaxpr/reduce_sum | solution.py:62
  679.7 4.3 fusion.71
  684.3 2.6 fusion.74
  686.9 36.1 %bitcast_add_fusion.3 = f32[256,2,12,128]{0,3,2,1:T(8,128)} fusion(f32[2,128,256,12]{2,1,3,0:T(8,128)S(1)} %fusion.74, f32[256,2,12,128]{0,3,2,1:T(8,128)} %get-tuple-element.277, f32[2,4096,256,12]{2,1,3,0:T(8,128)} %get-tuple-element.257, f32[256,2,12]{0,2,1:T(8,128)S(1)} %maximum_maximum_fusion.2, ...), kind=kOutput, calls=%fused_computation.13.clone.1 | convolution fusion | flops 6521094144 | bytes 112246792 | tf_op jit(solution)/shard_map/while/body/eval_jaxpr/tngk,knd->tngd/dot_general | solution.py:64
  724.4 5.2 fusion.70
  729.5 36.4 %bitcast_reduce_fusion.2 = (f32[256,2,12]{0,2,1:T(8,128)S(1)}, f32[2,4096,256,12]{2,1,3,0:T(8,128)}) fusion(bf16[256,2,12,128]{3,0,2,1:T(8,128)(2,1)} %get-tuple-element.293, bf16[8,4096,2,128]{3,1,0,2:T(8,128)(2,1)} %get-tuple-element.292, s32[]{:T(128)S(6)} %copy.71), kind=kOutput, calls=%fused_computation.2.clone.1 | convolution fusion | flops 6492776448 | bytes 104357888 | tf_op jit(solution)/shard_map/while/body/eval_jaxpr/tngd,knd->tngk/dot_general | solution.py:53
  766.0 31.1 %fusion.72 = f32[256,2,12]{0,2,1:T(8,128)S(1)} fusion(f32[2,4096,256,12]{2,1,3,0:T(8,128)} %get-tuple-element.257, f32[256,2,12]{0,2,1:T(8,128)S(1)} %maximum_maximum_fusion.2), kind=kLoop, calls=%fused_computation.5.clone.1 | loop fusion | flops 75491328 | bytes 100712448 | tf_op jit(solution)/shard_map/while/body/eval_jaxpr/reduce_sum | solution.py:62
  797.1 4.3 fusion.71
  801.6 2.6 fusion.74
  804.3 36.1 %bitcast_add_fusion.3 = f32[256,2,12,128]{0,3,2,1:T(8,128)} fusion(f32[2,128,256,12]{2,1,3,0:T(8,128)S(1)} %fusion.74, f32[256,2,12,128]{0,3,2,1:T(8,128)} %get-tuple-element.277, f32[2,4096,256,12]{2,1,3,0:T(8,128)} %get-tuple-element.257, f32[256,2,12]{0,2,1:T(8,128)S(1)} %maximum_maximum_fusion.2, ...), kind=kOutput, calls=%fused_computation.13.clone.1 | convolution fusion | flops 6521094144 | bytes 112246792 | tf_op jit(solution)/shard_map/while/body/eval_jaxpr/tngk,knd->tngd/dot_general | solution.py:64
  841.7 5.2 fusion.70
  846.9 36.4 %bitcast_reduce_fusion.2 = (f32[256,2,12]{0,2,1:T(8,128)S(1)}, f32[2,4096,256,12]{2,1,3,0:T(8,128)}) fusion(bf16[256,2,12,128]{3,0,2,1:T(8,128)(2,1)} %get-tuple-element.293, bf16[8,4096,2,128]{3,1,0,2:T(8,128)(2,1)} %get-tuple-element.292, s32[]{:T(128)S(6)} %copy.71), kind=kOutput, calls=%fused_computation.2.clone.1 | convolution fusion | flops 6492776448 | bytes 104357888 | tf_op jit(solution)/shard_map/while/body/eval_jaxpr/tngd,knd->tngk/dot_general | solution.py:53
  883.3 31.1 %fusion.72 = f32[256,2,12]{0,2,1:T(8,128)S(1)} fusion(f32[2,4096,256,12]{2,1,3,0:T(8,128)} %get-tuple-element.257, f32[256,2,12]{0,2,1:T(8,128)S(1)} %maximum_maximum_fusion.2), kind=kLoop, calls=%fused_computation.5.clone.1 | loop fusion | flops 75491328 | bytes 100712448 | tf_op jit(solution)/shard_map/while/body/eval_jaxpr/reduce_sum | solution.py:62
  914.4 4.3 fusion.71
  919.0 2.6 fusion.74
  921.6 36.1 %bitcast_add_fusion.3 = f32[256,2,12,128]{0,3,2,1:T(8,128)} fusion(f32[2,128,256,12]{2,1,3,0:T(8,128)S(1)} %fusion.74, f32[256,2,12,128]{0,3,2,1:T(8,128)} %get-tuple-element.277, f32[2,4096,256,12]{2,1,3,0:T(8,128)} %get-tuple-element.257, f32[256,2,12]{0,2,1:T(8,128)S(1)} %maximum_maximum_fusion.2, ...), kind=kOutput, calls=%fused_computation.13.clone.1 | convolution fusion | flops 6521094144 | bytes 112246792 | tf_op jit(solution)/shard_map/while/body/eval_jaxpr/tngk,knd->tngd/dot_general | solution.py:64
  959.0 5.2 fusion.70
  964.2 36.4 %bitcast_reduce_fusion.2 = (f32[256,2,12]{0,2,1:T(8,128)S(1)}, f32[2,4096,256,12]{2,1,3,0:T(8,128)}) fusion(bf16[256,2,12,128]{3,0,2,1:T(8,128)(2,1)} %get-tuple-element.293, bf16[8,4096,2,128]{3,1,0,2:T(8,128)(2,1)} %get-tuple-element.292, s32[]{:T(128)S(6)} %copy.71), kind=kOutput, calls=%fused_computation.2.clone.1 | convolution fusion | flops 6492776448 | bytes 104357888 | tf_op jit(solution)/shard_map/while/body/eval_jaxpr/tngd,knd->tngk/dot_general | solution.py:53
  1000.6 31.1 %fusion.72 = f32[256,2,12]{0,2,1:T(8,128)S(1)} fusion(f32[2,4096,256,12]{2,1,3,0:T(8,128)} %get-tuple-element.257, f32[256,2,12]{0,2,1:T(8,128)S(1)} %maximum_maximum_fusion.2), kind=kLoop, calls=%fused_computation.5.clone.1 | loop fusion | flops 75491328 | bytes 100712448 | tf_op jit(solution)/shard_map/while/body/eval_jaxpr/reduce_sum | solution.py:62
  1031.7 4.3 fusion.71
  1036.3 2.6 fusion.74
  1039.0 36.1 %bitcast_add_fusion.3 = f32[256,2,12,128]{0,3,2,1:T(8,128)} fusion(f32[2,128,256,12]{2,1,3,0:T(8,128)S(1)} %fusion.74, f32[256,2,12,128]{0,3,2,1:T(8,128)} %get-tuple-element.277, f32[2,4096,256,12]{2,1,3,0:T(8,128)} %get-tuple-element.257, f32[256,2,12]{0,2,1:T(8,128)S(1)} %maximum_maximum_fusion.2, ...), kind=kOutput, calls=%fused_computation.13.clone.1 | convolution fusion | flops 6521094144 | bytes 112246792 | tf_op jit(solution)/shard_map/while/body/eval_jaxpr/tngk,knd->tngd/dot_general | solution.py:64
  1076.4 5.2 fusion.70
  1081.6 36.4 %bitcast_reduce_fusion.2 = (f32[256,2,12]{0,2,1:T(8,128)S(1)}, f32[2,4096,256,12]{2,1,3,0:T(8,128)}) fusion(bf16[256,2,12,128]{3,0,2,1:T(8,128)(2,1)} %get-tuple-element.293, bf16[8,4096,2,128]{3,1,0,2:T(8,128)(2,1)} %get-tuple-element.292, s32[]{:T(128)S(6)} %copy.71), kind=kOutput, calls=%fused_computation.2.clone.1 | convolution fusion | flops 6492776448 | bytes 104357888 | tf_op jit(solution)/shard_map/while/body/eval_jaxpr/tngd,knd->tngk/dot_general | solution.py:53
  1118.0 31.1 %fusion.72 = f32[256,2,12]{0,2,1:T(8,128)S(1)} fusion(f32[2,4096,256,12]{2,1,3,0:T(8,128)} %get-tuple-element.257, f32[256,2,12]{0,2,1:T(8,128)S(1)} %maximum_maximum_fusion.2), kind=kLoop, calls=%fused_computation.5.clone.1 | loop fusion | flops 75491328 | bytes 100712448 | tf_op jit(solution)/shard_map/while/body/eval_jaxpr/reduce_sum | solution.py:62
  1149.1 4.3 fusion.71
  1153.7 2.6 fusion.74
  1156.3 36.1 %bitcast_add_fusion.3 = f32[256,2,12,128]{0,3,2,1:T(8,128)} fusion(f32[2,128,256,12]{2,1,3,0:T(8,128)S(1)} %fusion.74, f32[256,2,12,128]{0,3,2,1:T(8,128)} %get-tuple-element.277, f32[2,4096,256,12]{2,1,3,0:T(8,128)} %get-tuple-element.257, f32[256,2,12]{0,2,1:T(8,128)S(1)} %maximum_maximum_fusion.2, ...), kind=kOutput, calls=%fused_computation.13.clone.1 | convolution fusion | flops 6521094144 | bytes 112246792 | tf_op jit(solution)/shard_map/while/body/eval_jaxpr/tngk,knd->tngd/dot_general | solution.py:64
  1192.4 2.3 divide_convert_fusion
  1194.6 16.5 %fusion.47 = f32[256,5120]{1,0:T(8,128)} fusion(bf16[256,3072]{0,1:T(8,128)(2,1)S(1)} %bitcast.123, bf16[3072,5120]{1,0:T(8,128)(2,1)} %param.17), kind=kOutput, calls=%fused_computation.73 | convolution fusion | flops 8053063680 | bytes 38273024 | tf_op jit(solution)/shard_map/dot_general | solution.py:72
  1214.8 101.0 %all-reduce.2.cloned.1.call-done = f32[256,5120]{1,0:T(8,128)} async-done(((f32[256,5120]{1,0:T(8,128)}), f32[256,5120]{1,0:T(8,128)}) %all-reduce.2.cloned.1.call-update) | async-done | bytes 5242896 | tf_op jit(solution)/shard_map/psum | solution.py:73
  1315.8 4.7 fusion.42
  (118 shorter events, 25.9 us)
Async XLA Ops:
  7.2 54.2 %all-gather.14.cloned.1.call-start = ((), (), s32[]{:S(2)}) async-start(), calls=%async_computation.4 | async-start | bytes 1179648 | tf_op jit(solution)/shard_map/all_gather | solution.py:45
  29.4 8.1 copy-start.6
  29.4 9.9 copy-start.2
  36.4 48.7 %all-gather.8.cloned.1.call-start = ((), (), s32[]{:S(2)}) async-start(), calls=%async_computation | async-start | bytes 1179648 | tf_op jit(solution)/shard_map/all_gather | solution.py:44
  37.4 0.7 copy-start.3
  37.8 0.6 copy-start.4
  39.2 130.5 %all-gather.10.cloned.1.call-start = ((), (), s32[]{:S(2)}) async-start(), calls=%async_computation.2 | async-start | bytes 18874368 | tf_op jit(solution)/shard_map/all_gather | solution.py:42
  41.0 213.4 %all-gather.12.cloned.1.call-start = ((), (), s32[]{:S(2)}) async-start(), calls=%async_computation.3 | async-start | bytes 18874368 | tf_op jit(solution)/shard_map/all_gather | solution.py:43
  44.3 1271.5 %all-reduce.2.cloned.1.call-start = ((), (), s32[]{:S(2)}) async-start(), calls=%async_computation.1 | async-start | bytes 10485760 | tf_op jit(solution)/shard_map/psum | solution.py:73
  328.5 4.6 copy-start
  445.0 4.6 copy-start
  562.4 4.6 copy-start
  679.7 4.6 copy-start
  797.0 4.6 copy-start
  914.4 4.6 copy-start
  1031.7 4.6 copy-start
  1149.1 4.6 copy-start
  1211.1 2.9 copy-start.5
  1211.1 104.7 %copy-start.1 = (bf16[256,5120]{1,0:T(8,128)(2,1)S(1)}, bf16[256,5120]{1,0:T(8,128)(2,1)}, u32[]{:S(2)}) copy-start(bf16[256,5120]{1,0:T(8,128)(2,1)} %param.10) | copy-start | bytes 7864324
Sparse Core Ops, SparseCore 0:
  36.5 24.8 all-gather.13
  63.6 21.4 all-gather.7
  87.2 82.4 all-gather.9
  171.2 83.1 all-gather.11
  1211.3 104.4 all-reduce.1
where the time goes:
time: 1330 us
  matrix products  676 us (51%)
  waiting for transfers between devices  301 us (23%)
  other arithmetic  297 us (22%)
  local copies, waits for them, and re-layouts  33.8 us (3%)
  between operations  14 us (1%)
    dot_general x8, matrix products, attend(): jnp.einsum('tngd,knd->tngk', queries, kp_block, preferred_element_type=jn...  291 us
    dot_general x8, matrix products, attend(): jnp.einsum('tngk,knd->tngd', p_pref.astype(jnp.bfloat16), vp_block, prefe...  288 us
    reduce_sum x16, other arithmetic, attend(): run_sum = run_sum * rescale + p_pref.sum(axis=-1) + p_recent.sum(axis=-1)  283 us
    psum x1, waiting for transfers between devices, local_step(): y = (x_f32 + lax.psum(proj_part, 'tp')).astype(jnp.bfloat16)  101 us
    all_gather x1, waiting for transfers between devices, local_step(): k_prefix = lax.all_gather(k_cache, 'cp')  84.7 us
    all_gather x1, waiting for transfers between devices, local_step(): v_prefix = lax.all_gather(v_cache, 'cp')  84.6 us
    dot_general x8, matrix products, attend(): jnp.einsum('tngd,knd->tngk', queries, kr_block, preferred_element_type=jn...  41.4 us
  transfers between devices with their start and end apart: 5, of which 5 were waited for; matrix products, arithmetic and copies ran while one was open for 2% of the time, Pallas kernels for 0%

commit v1 on v0

v1 whole, which is shorter than its diff:
```python
import functools
import math

import jax
import jax.numpy as jnp
from jax import lax
from jax.experimental import pallas as pl
from jax.experimental.pallas import tpu as pltpu
from jax.sharding import PartitionSpec as P

EPS = 1.5625e-07
MASK_VALUE = -1e30
LANES = 128
SUB = 256
NC = 512
PHASE_TOKENS = 128
CHUNKS = 4
MESH = pl.DeviceIdType.MESH
F32 = jnp.float32
BF16 = jnp.bfloat16


def dot(a, b, dims=(((1,), (0,)), ((), ()))):
    return lax.dot_general(a, b, dims, preferred_element_type=F32)


def relayout_kernel(k_ref, v_ref, out_ref):
    rows = 2 * LANES
    wide = lax.broadcasted_iota(jnp.int32, (rows, rows), 0)
    tall = lax.broadcasted_iota(jnp.int32, (rows, rows), 1)
    pick = (wide // 2 + (wide % 2) * LANES == tall).astype(BF16)
    pick_t = (tall // 2 + (tall % 2) * LANES == wide).astype(BF16)
    for i in range(k_ref.shape[0] // rows):
        here = slice(i * LANES, (i + 1) * LANES)
        keys = dot(pick_t, k_ref[i * rows:(i + 1) * rows, :]).astype(BF16)
        vals = dot(v_ref[i * rows:(i + 1) * rows, :], pick, (((0,), (0,)), ((), ()))).astype(BF16)
        for g in range(2):
            out_ref[0, g, 0, here, :] = keys[g * LANES:(g + 1) * LANES, :]
            out_ref[0, g, 1, here, :] = vals[:, g * LANES:(g + 1) * LANES]


def relayout_cache(k_cache, v_cache):
    positions, groups, head_dim = k_cache.shape
    part = positions // CHUNKS
    flat = (positions * groups, head_dim)
    in_spec = pl.BlockSpec((part * groups, head_dim), lambda i: (i, 0))
    return pl.pallas_call(
        relayout_kernel,
        grid=(CHUNKS,),
        in_specs=[in_spec, in_spec],
        out_specs=pl.BlockSpec((1, groups, 2, part, head_dim), lambda i: (i, 0, 0, 0, 0)),
        out_shape=jax.ShapeDtypeStruct((CHUNKS, groups, 2, part, head_dim), BF16),
        compiler_params=pltpu.CompilerParams(vmem_limit_bytes=40 << 20),
        name="relayout",
    )(k_cache.reshape(flat), v_cache.reshape(flat))


def project_kernel(pairs_per_group, x_ref, g_ref, w_ref, b_ref, table_ref, qt_ref, kvn_ref, kn_ref, vn_ref, hid_ref, cos_ref, sin_ref):
    step = pl.program_id(0)
    tok = x_ref.shape[0]
    pair_count = table_ref.shape[1] // 2
    lane = lax.broadcasted_iota(jnp.int32, (tok, LANES), 1)

    @pl.when(step == 0)
    def _():
        x = x_ref[...].astype(F32)
        inv_rms = lax.rsqrt(jnp.mean(x * x, axis=-1, keepdims=True) + EPS)
        hid_ref[...] = (x * inv_rms * g_ref[...].astype(F32)).astype(BF16)
        table = jnp.concatenate([table_ref[...], jnp.zeros((tok, LANES - 2 * pair_count), F32)], axis=1)
        at = jnp.where(lane < 2 * pair_count, lane // 2, 0)
        cos_ref[...] = jnp.take_along_axis(table, at, axis=1)
        sin = jnp.take_along_axis(table, at + pair_count, axis=1)
        sin_ref[...] = jnp.where(lane % 2 == 0, -sin, sin)

    def rotate(head):
        swapped = jnp.where(lane % 2 == 0, pltpu.roll(head, LANES - 1, 1), pltpu.roll(head, 1, 1))
        turned = head * cos_ref[...] + swapped * sin_ref[...]
        return jnp.where(lane < 2 * pair_count, turned, head)

    both = dot(hid_ref[...], w_ref[...]) + b_ref[...].astype(F32)
    first, second = both[:, :LANES], both[:, LANES:]
    kind = lax.rem(step, pairs_per_group)

    @pl.when(kind < pairs_per_group - 1)
    def _():
        for j, head in enumerate((first, second)):
            turned = rotate(head).T.astype(BF16)
            for p in range(tok // PHASE_TOKENS):
                qt_ref[0, p, 0, :, j * LANES:(j + 1) * LANES] = turned[:, p * PHASE_TOKENS:(p + 1) * PHASE_TOKENS]

    @pl.when(kind == pairs_per_group - 1)
    def _():
        keys = rotate(first).astype(BF16)
        kvn_ref[0, 0] = keys
        kn_ref[...] = keys
        vn_ref[...] = second.astype(BF16)
        for i in range(tok // LANES):
            here = slice(i * LANES, (i + 1) * LANES)
            kvn_ref[0, 1, here, :] = second[here, :].T.astype(BF16)


def project_new(x, rope_table, norm_gain, w_qkv, b_qkv, groups):
    tok, width = x.shape
    cols = w_qkv.shape[1]
    per_group = cols // groups // (2 * LANES)
    query_heads = cols // groups // LANES - 2
    phases = tok // PHASE_TOKENS
    heads_per_tile = NC // PHASE_TOKENS
    tiles = query_heads // heads_per_tile
    steps_per_tile = heads_per_tile // 2

    def qt_map(i):
        j = jnp.minimum(i % per_group, per_group - 2)
        return (i // per_group, 0, j // steps_per_tile, 0, j % steps_per_tile)

    full = lambda shape: pl.BlockSpec(shape, lambda i: (0,) * len(shape))
    return pl.pallas_call(
        functools.partial(project_kernel, per_group),
        grid=(groups * per_group,),
        in_specs=[
            full((tok, width)),
            full((1, width)),
            pl.BlockSpec((width, 2 * LANES), lambda i: (0, i)),
            pl.BlockSpec((1, 2 * LANES), lambda i: (0, i)),
            full(rope_table.shape),
        ],
        out_specs=[
            pl.BlockSpec((1, phases, 1, LANES, 2 * LANES), qt_map),
            pl.BlockSpec((1, 2, tok, LANES), lambda i: (i // per_group, 0, 0, 0)),
            pl.BlockSpec((tok, LANES), lambda i: (0, i // per_group)),
            pl.BlockSpec((tok, LANES), lambda i: (0, i // per_group)),
        ],
        out_shape=[
            jax.ShapeDtypeStruct((groups, phases, tiles, LANES, NC), BF16),
            jax.ShapeDtypeStruct((groups, 2, tok, LANES), BF16),
            jax.ShapeDtypeStruct((tok, groups * LANES), BF16),
            jax.ShapeDtypeStruct((tok, groups * LANES), BF16),
        ],
        scratch_shapes=[pltpu.VMEM((tok, width), BF16), pltpu.VMEM((tok, LANES), F32), pltpu.VMEM((tok, LANES), F32)],
        compiler_params=pltpu.CompilerParams(vmem_limit_bytes=40 << 20),
        name="project",
    )(x, norm_gain.reshape(1, width), w_qkv, b_qkv.reshape(1, cols), rope_table)


def attention_kernel(n, heads, phases, qt_ref, kv_ref, kvn_ref, o_ref, ring_ref, ringn_ref,
                     k_buf, v_buf, s_ref, p_ref, acc_ref, m_ref, l_ref, mc_ref, al_ref, bias_ref,
                     fetch_sem, newest_sem, own_send, pair_send, hop_send, new_send, recv, new_recv):
    me = lax.axis_index("cp")
    pair = me + 1 - 2 * lax.rem(me, 2)
    right, left = lax.rem(me + 2, n), lax.rem(me + n - 2, n)
    groups, part = kv_ref.shape[1], kv_ref.shape[3]
    tok = kvn_ref.shape[2]
    span = CHUNKS * part
    span_new = n * tok
    sets = n
    per_group = qt_ref.shape[0] // groups
    spare = qt_ref.shape[0]
    scale = LANES ** -0.5 * math.log2(math.e)

    def remote(src, dst, send, got, where):
        return pltpu.make_async_remote_copy(src_ref=src, dst_ref=dst, send_sem=send, recv_sem=got, device_id={"cp": where}, device_id_type=MESH)

    def own_pair(c):
        return remote(kv_ref.at[c], ring_ref.at[1, c], own_send.at[0, c], recv.at[1, c], pair)

    def own_right(c):
        return remote(kv_ref.at[c], ring_ref.at[2 + c, 0], own_send.at[1, c], recv.at[2 + c, 0], right)

    def own_left(c):
        return remote(kv_ref.at[c], ring_ref.at[2 + c, 1], own_send.at[2, c], recv.at[2 + c, 1], left)

    def to_pair(s, side):
        return remote(ring_ref.at[s, side], ring_ref.at[s, 2 + side], pair_send.at[s, side], recv.at[s, 2 + side], pair)

    def hop_right(s):
        return remote(ring_ref.at[s, 0], ring_ref.at[s + 4, 0], hop_send.at[s], recv.at[s + 4, 0], right)

    def hop_left(s):
        return remote(ring_ref.at[s, 1], ring_ref.at[s + 2, 1], hop_send.at[s], recv.at[s + 2, 1], left)

    def new_copy(source, send, got, where, own=False):
        src = kvn_ref if own else ringn_ref.at[source]
        return remote(src, ringn_ref.at[source], new_send.at[send], new_recv.at[got], where)

    far = lax.rem(me + 4, n)
    new_right = new_copy(me, 0, 0, right, own=True)
    new_left = new_copy(me, 1, 1, left, own=True)
    new_pair = new_copy(me, 2, 3, pair, own=True)
    new_hop = new_copy(left, 3, 2, right)
    new_left_pair = new_copy(left, 4, 4, pair)
    new_right_pair = new_copy(right, 5, 5, pair)
    new_far_pair = new_copy(far, 6, 6, pair)

    barrier = pltpu.get_barrier_semaphore()
    for other in (pair, right, left):
        pl.semaphore_signal(barrier, inc=1, device_id={"cp": other}, device_id_type=MESH)
    pl.semaphore_wait(barrier, 3)
    for c in range(CHUNKS):
        own_right(c).start()
        own_left(c).start()
        own_pair(c).start()
    for copy in (new_right, new_left, new_pair):
        copy.start()

    def fetch_copies(source, slot, g):
        copies = []
        for c in range(CHUNKS):
            here = pl.ds(c * part, part)
            copies.append(pltpu.make_async_copy(source(c).at[g, 0], k_buf.at[slot, here], fetch_sem.at[slot, 0, c]))
            copies.append(pltpu.make_async_copy(source(c).at[g, 1], v_buf.at[slot, here], fetch_sem.at[slot, 1, c]))
        return copies

    def fetch_new(act):
        for g in range(groups):
            for j in range(n):
                here = pl.ds(g * span_new + j * tok, tok)

                def both(source):
                    for kind, buf in ((0, k_buf), (1, v_buf)):
                        copy = pltpu.make_async_copy(source.at[g, kind], buf.at[0, here], newest_sem.at[kind, g, j])
                        getattr(copy, act)()

                if act == "wait":
                    both(kvn_ref)
                else:
                    pl.when(j == me)(lambda: both(kvn_ref))
                    pl.when(j != me)(lambda: both(ringn_ref.at[j]))

    own = lambda c: kv_ref.at[c]
    for copy in fetch_copies(own, 0, 0):
        copy.start()

    row = lax.broadcasted_iota(jnp.int32, (tok, NC), 0)
    col = lax.rem(lax.broadcasted_iota(jnp.int32, (tok, NC), 1), PHASE_TOKENS)
    bias_ref[0] = jnp.zeros((tok, NC), F32)
    for p in range(phases):
        bias_ref[1 + p] = jnp.where(row <= col + p * PHASE_TOKENS, 0.0, MASK_VALUE)
    bias_ref[1 + phases] = jnp.full((tok, NC), MASK_VALUE, F32)

    m_ref[...] = jnp.full(m_ref.shape, MASK_VALUE, F32)
    l_ref[...] = jnp.zeros(l_ref.shape, F32)
    acc_ref[...] = jnp.zeros(acc_ref.shape, F32)
    s_ref[...] = jnp.zeros(s_ref.shape, F32)
    p_ref[...] = jnp.zeros(p_ref.shape, BF16)
    mc_ref[...] = jnp.zeros(mc_ref.shape, F32)
    al_ref[...] = jnp.ones(al_ref.shape, F32)

    def step(a=None, b=None, c=None):
        alpha_b, alpha_c = al_ref[0], al_ref[1]
        shift = mc_ref[...]
        run = {"max": None, "sum": None, "out": None}

        def scores(i):
            keys = k_buf[a["slot"], pl.ds(a["base"] + i * SUB, SUB), :]
            s = dot(keys, qt_ref[a["tile"]])
            if a["new"]:
                edge = 1 + lax.rem(a["tile"], per_group) // (per_group // phases)
                which = jnp.where(i < me, 0, jnp.where(i == me, edge, 1 + phases))
                s = s + bias_ref[which]
            s_ref[i * SUB:(i + 1) * SUB, :] = s
            top = jnp.max(s.reshape(SUB // 8, 8, NC), axis=0)
            run["max"] = top if run["max"] is None else jnp.maximum(run["max"], top)

        def weights(i):
            s = s_ref[i * SUB:(i + 1) * SUB, :]
            e = jnp.exp2((s * scale).reshape(SUB // 8, 8, NC) - shift[None])
            part_sum = jnp.sum(e, axis=0)
            run["sum"] = part_sum if run["sum"] is None else run["sum"] + part_sum
            p_ref[i * SUB:(i + 1) * SUB, :] = e.reshape(SUB, NC).astype(BF16)

        def values(i):
            at = c["base"] + i * SUB
            block = jnp.concatenate([v_buf[c["slot"], pl.ds(at + h * LANES, LANES), :] for h in range(SUB // LANES)], axis=1)
            out = dot(block, p_ref[i * SUB:(i + 1) * SUB, :])
            run["out"] = out if run["out"] is None else run["out"] + out

        stages = ((c, values), (b, weights), (a, scores))
        for i in range(max(spec["keys"] for spec, _ in stages if spec is not None) // SUB):
            for spec, stage in stages:
                if spec is not None and i < spec["keys"] // SUB:
                    stage(i)
        if c is not None:
            acc_ref[c["tile"]] = acc_ref[c["tile"]] * alpha_c + run["out"]
        if b is not None:
            l_ref[b["tile"]] = l_ref[b["tile"]] * alpha_b + run["sum"]
            al_ref[1] = alpha_b
        if a is not None:
            old = m_ref[a["tile"]]
            new = jnp.maximum(old, jnp.max(run["max"], axis=0, keepdims=True))
            m_ref[a["tile"]] = new
            mc_ref[...] = jnp.broadcast_to(new * scale, mc_ref.shape)
            al_ref[0] = jnp.exp2((old - new) * scale)

    def main(tile, slot):
        return {"tile": tile, "slot": slot, "base": 0, "keys": span, "new": False}

    def recent(at):
        return {"tile": at, "slot": 0, "base": at // per_group * span_new, "keys": span_new, "new": True}

    def one_set(st, _):
        for g in range(groups):
            for copy in fetch_copies(own, g, g):
                copy.wait()
            if g == groups - 1:
                nxt = st + 1

                @pl.when((st >= 1) & (st <= sets - 2))
                def _():
                    remote(kv_ref.at[0], ring_ref.at[nxt, 0], own_send.at[0, 0], recv.at[nxt, 0], left).wait_recv()
                    to_pair(nxt, 0).start()
                    remote(kv_ref.at[0], ring_ref.at[nxt, 1], own_send.at[0, 0], recv.at[nxt, 1], right).wait_recv()
                    to_pair(nxt, 1).start()

                @pl.when((st >= 1) & (st <= 2))
                def _():
                    hop_right(nxt).start()

                @pl.when((st >= 3) & (st <= 4))
                def _():
                    hop_left(nxt).start()

                @pl.when(st == sets - 3)
                def _():
                    new_copy(left, 0, 0, right).wait_recv()
                    new_hop.start()
                    new_left_pair.start()
                    new_copy(right, 0, 1, left).wait_recv()
                    new_right_pair.start()

                @pl.when(st == sets - 2)
                def _():
                    new_copy(far, 0, 2, right).wait_recv()
                    new_far_pair.start()

            def one_tile(t, _):
                @pl.when(t == per_group - 2)
                def _():
                    if g < groups - 1:
                        @pl.when(st == 0)
                        def _():
                            for copy in fetch_copies(own, g + 1, g + 1):
                                copy.start()

                        @pl.when(st > 0)
                        def _():
                            for copy in fetch_copies(lambda c: ring_ref.at[st, c], g + 1, g + 1):
                                copy.start()
                    else:
                        @pl.when(st == 0)
                        def _():
                            for c in range(CHUNKS):
                                own_pair(c).wait_recv()

                        @pl.when((st >= 1) & (st <= sets - 2))
                        def _():
                            for side in range(2):
                                to_pair(st + 1, side).wait_recv()

                        @pl.when(st <= sets - 2)
                        def _():
                            for copy in fetch_copies(lambda c: ring_ref.at[st + 1, c], 0, 0):
                                copy.start()

                before = (groups + g - 1) % groups
                early = (st == 0) & (g == 0)
                last = jnp.where(t >= 1, g * per_group + t - 1, jnp.where(early, spare, before * per_group + per_group - 1))
                older = jnp.where(t >= 2, g * per_group + t - 2, jnp.where(early, spare, before * per_group + per_group - 2 + t))
                step(main(g * per_group + t, g), main(last, 0), main(older, jnp.where(t >= 2, g, before)))
                return 0

            lax.fori_loop(0, per_group, one_tile, 0)
        return 0

    lax.fori_loop(0, sets, one_set, 0)

    for got in (3, 4, 5, 6):
        new_copy(pair, 0, got, pair).wait_recv()
    fetch_new("start")
    final = groups * per_group - 1
    fetch_new("wait")
    step(recent(0), main(final, 0), main(final - 1, groups - 1))
    step(recent(1), recent(0), main(final, groups - 1))

    def new_tile(t, _):
        step(recent(t), recent(t - 1), recent(t - 2))
        return 0

    lax.fori_loop(2, groups * per_group, new_tile, 0)
    step(None, recent(final), recent(final - 1))
    step(None, None, recent(final))

    heads_per_tile = NC // PHASE_TOKENS
    tiles = per_group // phases

    def finish(t, _):
        total = jnp.sum(l_ref[t], axis=0, keepdims=True)
        out = (acc_ref[t] / total).T.astype(BF16)
        g, p, h = t // per_group, lax.rem(t, per_group) // tiles, lax.rem(t, tiles)
        for i in range(heads_per_tile):
            at = pl.multiple_of((g * heads + h * heads_per_tile + i) * LANES, LANES)
            rows = pl.ds(pl.multiple_of(p * PHASE_TOKENS, PHASE_TOKENS), PHASE_TOKENS)
            o_ref[rows, pl.ds(at, LANES)] = out[i * PHASE_TOKENS:(i + 1) * PHASE_TOKENS, :]
        return 0

    lax.fori_loop(0, groups * per_group, finish, 0)

    for c in range(CHUNKS):
        own_right(c).wait_send()
        own_left(c).wait_send()
        own_pair(c).wait_send()
    for s in range(2, sets):
        for side in range(2):
            to_pair(s, side).wait_send()
    for s in (2, 3):
        hop_right(s).wait_send()
    for s in (4, 5):
        hop_left(s).wait_send()
    for copy in (new_right, new_left, new_pair, new_hop, new_left_pair, new_right_pair, new_far_pair):
        copy.wait_send()


def attend(qt, kv, kvn, n, heads):
    groups, phases, tiles = qt.shape[:3]
    part, tok = kv.shape[3], kvn.shape[2]
    span, span_new = CHUNKS * part, n * tok
    count = groups * phases * tiles
    rows = max(span, groups * span_new)
    any_spec = pl.BlockSpec(memory_space=pl.ANY)
    vmem_spec = pl.BlockSpec(memory_space=pltpu.VMEM)
    dma = pltpu.SemaphoreType.DMA
    flops = 4 * count * NC * LANES * n * (span + tok)
    out = pl.pallas_call(
        functools.partial(attention_kernel, n, heads, phases),
        in_specs=[vmem_spec, any_spec, any_spec],
        out_specs=[vmem_spec, any_spec, any_spec],
        out_shape=[
            jax.ShapeDtypeStruct((tok, groups * heads * LANES), BF16),
            jax.ShapeDtypeStruct((n,) + kv.shape, BF16),
            jax.ShapeDtypeStruct((n,) + kvn.shape, BF16),
        ],
        scratch_shapes=[
            pltpu.VMEM((groups, rows, LANES), BF16),
            pltpu.VMEM((groups, rows, LANES), BF16),
            pltpu.VMEM((max(span, span_new), NC), F32),
            pltpu.VMEM((max(span, span_new), NC), BF16),
            pltpu.VMEM((count + 1, LANES, NC), F32),
            pltpu.VMEM((count, 1, NC), F32),
            pltpu.VMEM((count + 1, 8, NC), F32),
            pltpu.VMEM((8, NC), F32),
            pltpu.VMEM((2, 1, NC), F32),
            pltpu.VMEM((2 + phases, tok, NC), F32),
            dma((groups, 2, CHUNKS)),
            dma((2, groups, n)),
            dma((3, CHUNKS)),
            dma((n, 2)),
            dma((n,)),
            dma((7,)),
            dma((n, CHUNKS)),
            dma((7,)),
        ],
        cost_estimate=pl.CostEstimate(flops=flops, bytes_accessed=4 * kv.size * n, transcendentals=flops // (4 * LANES)),
        compiler_params=pltpu.CompilerParams(collective_id=0, has_side_effects=True, vmem_limit_bytes=60 << 20),
        name="attend",
    )(qt.reshape((count,) + qt.shape[3:]), kv, kvn)
    return out[0]


OUT_COLS = 512


def output_kernel(n, o_ref, x_ref, w_ref, y_ref, w_buf, x_buf, full_buf, send_buf, got_buf, y_buf, w_sem, x_sem, part_send, part_recv, y_send, y_recv, y_sem):
    me = lax.axis_index("tp")
    tok, width = x_ref.shape
    rows = tok // n
    pieces = width // OUT_COLS
    slots = w_buf.shape[0]
    my_rows = pl.ds(pl.multiple_of(me * rows, rows), rows)

    def cols(k):
        return slice(k * OUT_COLS, (k + 1) * OUT_COLS)

    def weight(k):
        return pltpu.make_async_copy(w_ref.at[:, cols(k)], w_buf.at[k % slots], w_sem.at[k % slots])

    def partial(k, d):
        to = lax.rem(me + d, n)
        src = send_buf.at[k, pl.ds(pl.multiple_of(to * rows, rows), rows)]
        return pltpu.make_async_remote_copy(src_ref=src, dst_ref=got_buf.at[k, d - 1], send_sem=part_send.at[k, d - 1], recv_sem=part_recv.at[k, d - 1], device_id={"tp": to}, device_id_type=MESH)

    def result(k, d):
        to = lax.rem(me + d, n)
        return pltpu.make_async_remote_copy(src_ref=y_buf.at[k], dst_ref=y_ref.at[my_rows, cols(k)], send_sem=y_send.at[k, d - 1], recv_sem=y_recv.at[k, d - 1], device_id={"tp": to}, device_id_type=MESH)

    def local(k):
        return pltpu.make_async_copy(y_buf.at[k], y_ref.at[my_rows, cols(k)], y_sem.at[k])

    own_x = pltpu.make_async_copy(x_ref.at[my_rows], x_buf, x_sem)
    own_x.start()
    for k in range(slots):
        weight(k).start()
    barrier = pltpu.get_barrier_semaphore()
    for d in range(1, n):
        pl.semaphore_signal(barrier, inc=1, device_id={"tp": lax.rem(me + d, n)}, device_id_type=MESH)
    pl.semaphore_wait(barrier, n - 1)
    own_x.wait()
    for k in range(pieces + 4):
        if k < pieces:
            weight(k).wait()
            part = dot(o_ref[...], w_buf[k % slots])
            full_buf[k % 4] = part
            send_buf[k] = part.astype(BF16)
            if k + slots < pieces:
                weight(k + slots).start()
        if 1 <= k <= pieces:
            for d in range(1, n):
                partial(k - 1, d).start()
        if 3 <= k < pieces + 3:
            j = k - 3
            total = full_buf[j % 4, my_rows, :]
            for d in range(1, n):
                partial(j, d).wait_recv()
                total = total + got_buf[j, d - 1].astype(F32)
            y_buf[j] = (x_buf[:, cols(j)].astype(F32) + total).astype(BF16)
        if k >= 4:
            local(k - 4).start()
            for d in range(1, n):
                result(k - 4, d).start()
    for k in range(pieces):
        local(k).wait()
        for d in range(1, n):
            partial(k, d).wait_send()
            result(k, d).wait_send()
            result(k, d).wait_recv()


def project_out(o, x, w_out, n):
    tok, width = x.shape
    pieces = width // OUT_COLS
    rows = tok // n
    any_spec = pl.BlockSpec(memory_space=pl.ANY)
    vmem_spec = pl.BlockSpec(memory_space=pltpu.VMEM)
    dma = pltpu.SemaphoreType.DMA
    slots = 3
    return pl.pallas_call(
        functools.partial(output_kernel, n),
        in_specs=[vmem_spec, any_spec, any_spec],
        out_specs=any_spec,
        out_shape=jax.ShapeDtypeStruct((tok, width), BF16),
        scratch_shapes=[
            pltpu.VMEM((slots, o.shape[1], OUT_COLS), BF16),
            pltpu.VMEM((rows, width), BF16),
            pltpu.VMEM((4, tok, OUT_COLS), F32),
            pltpu.VMEM((pieces, tok, OUT_COLS), BF16),
            pltpu.VMEM((pieces, n - 1, rows, OUT_COLS), BF16),
            pltpu.VMEM((pieces, rows, OUT_COLS), BF16),
            dma((slots,)),
            dma,
            dma((pieces, n - 1)),
            dma((pieces, n - 1)),
            dma((pieces, n - 1)),
            dma((pieces, n - 1)),
            dma((pieces,)),
        ],
        cost_estimate=pl.CostEstimate(flops=2 * tok * o.shape[1] * width, bytes_accessed=2 * w_out.size, transcendentals=0),
        compiler_params=pltpu.CompilerParams(collective_id=1, has_side_effects=True, vmem_limit_bytes=40 << 20),
        name="project_out",
    )(o, x, w_out)


def local_step(cp, tp, x, k_cache, v_cache, rope_table, norm_gain, w_qkv, b_qkv, w_out):
    groups = k_cache.shape[1]
    heads = w_qkv.shape[1] // groups // LANES - 2
    kv = relayout_cache(k_cache, v_cache)
    qt, kvn, new_k, new_v = project_new(x, rope_table, norm_gain, w_qkv, b_qkv, groups)
    o = attend(qt, kv, kvn, cp, heads)
    y = project_out(o, x, w_out, tp)
    new_shape = (x.shape[0],) + k_cache.shape[1:]
    return y, new_k.reshape(new_shape), new_v.reshape(new_shape)


def solution(mesh):
    row_spec = P(("dp", "cp"), None)
    cache_spec = P(("dp", "cp"), "tp", None)
    body = functools.partial(local_step, mesh.shape["cp"], mesh.shape["tp"])
    return jax.shard_map(body, mesh=mesh, in_specs=(row_spec, cache_spec, cache_spec, row_spec, P(None), P(None, "tp"), P("tp"), P("tp", None)), out_specs=(row_spec, cache_spec, cache_spec), check_vma=False)
```

time: 1330 us -> 323 us (0.24)
  matrix products: 676 us -> 0 us
  Pallas kernels: 0 us -> 308 us
  waiting for transfers between devices: 301 us -> 0 us
  other arithmetic: 297 us -> 0 us
  local copies, waits for them, and re-layouts: 33.8 us -> 13.9 us
    dot_general x34 -> x0, matrix products: 676 us -> none  [the longest x8 291 us: attend(): jnp.einsum('tngd,knd->tngk', queries, kp_block, preferred_element_type=jn...]
    pallas_call x0 -> x4, Pallas kernels: none -> 308 us  [the longest x1 216 us: attend(): pl.pallas_call(functools.partial(attention_kernel, n, heads, phases), in_...]
    reduce_sum x17 -> x0, other arithmetic: 285 us -> none  [the longest x16 283 us: attend(): run_sum = run_sum * rescale + p_pref.sum(axis=-1) + p_recent.sum(axis=-1)]
    all_gather x4 -> x0, waiting for transfers between devices: 199 us -> none  [the longest x1 84.7 us: local_step(): k_prefix = lax.all_gather(k_cache, 'cp')]
    psum x1 -> x0, waiting for transfers between devices: 101 us -> none  [local_step(): y = (x_f32 + lax.psum(proj_part, 'tp')).astype(jnp.bfloat16)]
  transfers between devices with their start and end apart: 5 -> 0, of which waited for: 5 -> 0; matrix products, arithmetic and copies ran while one was open for 2% -> 0% of each run, Pallas kernels for 0% -> 0%
where the time goes in v1:
time: 323 us; the launch traced here: 322 us
  Pallas kernels  308 us (95%)
  local copies, waits for them, and re-layouts  13.9 us (4%)
    pallas_call x1, Pallas kernels, attend(): pl.pallas_call(functools.partial(attention_kernel, n, heads, phases), in_...  216 us
    pallas_call x1, Pallas kernels, project_out(): pl.pallas_call(functools.partial(output_kernel, n), in_specs=[vmem_spec,...  65.4 us
    pallas_call x1, Pallas kernels, project_new(): pl.pallas_call(functools.partial(project_kernel, per_group), grid=(groups...  23.7 us
    unnamed x18, local copies, waits for them, and re-layouts  11.1 us

profile of v1, /device:TPU:97, one launch (start us, length us, event | category | flops | bytes accessed | tf_op | source)
XLA Modules:
  0.0 322.2 jit_solution(4104655561572875306)
XLA Ops:
  0.6 0.7 reshape.28.b_ref
  1.3 0.7 reshape.27.g_ref
  2.1 0.9 copy.11.table_ref
  3.0 0.0 copy-start
  3.0 1.7 copy-done
  4.7 0.0 copy-start.3
  4.7 23.7 %project.1 = (bf16[2,2,3,128,512]{4,3,2,1,0:T(8,128)(2,1)S(1)}, bf16[2,2,256,128]{3,2,1,0:T(8,128)(2,1)S(1)}, bf16[256,256]{1,0:T(8,128)(2,1)S(1)}, bf16[256,256]{1,0:T(8,128)(2,1)S(1)}) custom-call(bf16[256,5120]{1,0:T(8,128)(2,1)S(1)} %copy-done, bf16[1,5120]{1,0:T(2,128)(2,1)S(1)} %reshape.27.g_ref, bf16[5120,3584]{1,0:T(8,128)(2,1)} %w_ref.2, ...), custom_call_target="tpu_custom_call" | custom-call | tf_op jit(solution)/shard_map/project/pallas_call | solution.py:117
  28.5 0.0 copy-start.6
  28.5 1.1 copy-done.6
  29.6 0.0 copy-start.7
  29.6 0.7 copy-done.7
  30.3 0.7 reshape.32
  31.0 0.7 reshape.33
  31.7 0.0 copy-done.3
  31.7 0.0 copy-start.4
  31.7 1.6 copy-done.4
  33.3 2.5 relayout.1.kv_ref
  35.8 0.0 copy-start.2
  35.8 2.1 copy-done.2
  37.9 0.0 copy-start.1
  37.9 216.0 %attend.1 = (bf16[256,3072]{1,0:T(8,128)(2,1)}, bf16[8,4,2,2,1024,128]{5,4,3,2,1,0:T(8,128)(2,1)}, bf16[8,2,2,256,128]{4,3,2,1,0:T(8,128)(2,1)}) custom-call(bf16[12,128,512]{2,1,0:T(8,128)(2,1)} %bitcast.5, bf16[4,2,2,1024,128]{4,3,2,1,0:T(8,128)(2,1)} %copy-done.2, bf16[2,2,256,128]{3,2,1,0:T(8,128)(2,1)} %copy-done.7), custom_call_target="tpu_custom_call" | custom-call | flops 109521666048 | bytes 67108864 | tf_op jit(solution)/shard_map/attend/pallas_call | solution.py:432
  253.8 0.0 copy-done.1
  253.9 0.0 copy-start.5
  253.9 1.4 copy-done.5
  255.3 65.4 %project_out.1 = bf16[256,5120]{1,0:T(8,128)(2,1)S(1)} custom-call(bf16[256,3072]{1,0:T(8,128)(2,1)S(1)} %copy-done.5, bf16[256,5120]{1,0:T(8,128)(2,1)S(1)} %copy-done.1, bf16[3072,5120]{1,0:T(8,128)(2,1)} %w_ref.3), custom_call_target="tpu_custom_call" | custom-call | flops 8053063680 | bytes 31457280 | tf_op jit(solution)/shard_map/project_out/pallas_call | solution.py:544
  320.7 1.5 copy.13
Async XLA Ops:
  3.0 1.7 copy-start
  4.7 27.0 %copy-start.3 = (bf16[4096,2,128]{2,1,0:T(2,128)(2,1)S(1)}, bf16[4096,2,128]{2,1,0:T(2,128)(2,1)}, u32[]{:S(2)}) copy-start(bf16[4096,2,128]{2,1,0:T(2,128)(2,1)} %param.9) | copy-start | bytes 6291460
  28.5 1.1 copy-start.6
  29.6 0.7 copy-start.7
  31.7 1.6 copy-start.4
  35.8 2.1 copy-start.2
  37.9 216.0 %copy-start.1 = (bf16[256,5120]{1,0:T(8,128)(2,1)S(1)}, bf16[256,5120]{1,0:T(8,128)(2,1)}, u32[]{:S(2)}) copy-start(bf16[256,5120]{1,0:T(8,128)(2,1)} %x_ref.3) | copy-start | bytes 7864324
  253.9 1.4 copy-start.5

commit v2 on v0

v2 whole, which is shorter than its diff:
```python
import functools
import math

import jax
import jax.numpy as jnp
from jax import lax
from jax.experimental import pallas as pl
from jax.experimental.pallas import tpu as pltpu
from jax.sharding import PartitionSpec as P

EPS = 1.5625e-07
MASK_VALUE = -1e30
LANES = 128
SUB = 256
NC = 512
PHASE_TOKENS = 128
CHUNKS = 4
COLS = 512
OUT_SLOTS = 6
MESH = pl.DeviceIdType.MESH
F32 = jnp.float32
BF16 = jnp.bfloat16
DMA = pltpu.SemaphoreType.DMA


def dot(a, b, dims=(((1,), (0,)), ((), ()))):
    return lax.dot_general(a, b, dims, preferred_element_type=F32)


def block_kernel(dims, x_ref, kc_ref, vc_ref, table_ref, g_ref, wq_ref, b_ref, wo_ref,
                 y_ref, kn_ref, vn_ref, ring_ref, ringn_ref,
                 k_buf, v_buf, stage, kvn, qt_ref, hid_ref, x_buf, w_buf, a_buf, cos_ref, sin_ref, kn_buf, vn_buf,
                 s_ref, p_ref, acc_ref, m_ref, l_ref, mc_ref, al_ref, bias_ref,
                 o_buf, res_buf, full_buf, mine_buf, send_buf, got_buf, y_buf,
                 in_sem, w_sem, out_sem, fetch_sem, newest_sem, own_send, pair_send, hop_send, new_send, recv, new_recv,
                 part_send, part_recv, y_send, y_recv, y_sem):
    n, ranks, groups, heads = dims
    me = lax.axis_index("cp")
    rank = lax.axis_index("tp")
    pair = me + 1 - 2 * lax.rem(me, 2)
    right, left, far = lax.rem(me + 2, n), lax.rem(me + n - 2, n), lax.rem(me + 4, n)
    tok, width = x_ref.shape
    part = stage.shape[3]
    span, span_new = CHUNKS * part, n * tok
    phases = tok // PHASE_TOKENS
    heads_per_tile = NC // PHASE_TOKENS
    tiles = heads // heads_per_tile
    per_group = phases * tiles
    count = groups * per_group
    spare = count
    half = kc_ref.shape[0] // 2
    scale = LANES ** -0.5 * math.log2(math.e)
    head_count = groups * (heads + 2)
    w_blocks = head_count * LANES // COLS
    heads_per_block = COLS // LANES
    pieces = width // COLS
    out_depth = wo_ref.shape[0]
    rows = PHASE_TOKENS // ranks

    def remote(src, dst, send, got, axis, where):
        return pltpu.make_async_remote_copy(src_ref=src, dst_ref=dst, send_sem=send, recv_sem=got, device_id={axis: where}, device_id_type=MESH)

    def own_pair(c):
        return remote(stage.at[c], ring_ref.at[1, c], own_send.at[0, c], recv.at[1, c], "cp", pair)

    def own_right(c):
        return remote(stage.at[c], ring_ref.at[2 + c, 0], own_send.at[1, c], recv.at[2 + c, 0], "cp", right)

    def own_left(c):
        return remote(stage.at[c], ring_ref.at[2 + c, 1], own_send.at[2, c], recv.at[2 + c, 1], "cp", left)

    def to_pair(s, side):
        return remote(ring_ref.at[s, side], ring_ref.at[s, 2 + side], pair_send.at[s, side], recv.at[s, 2 + side], "cp", pair)

    def from_side(s, side):
        return remote(stage.at[0], ring_ref.at[s, side], own_send.at[0, 0], recv.at[s, side], "cp", pair)

    def hop_right(s):
        return remote(ring_ref.at[s, 0], ring_ref.at[s + 4, 0], hop_send.at[s], recv.at[s + 4, 0], "cp", right)

    def hop_left(s):
        return remote(ring_ref.at[s, 1], ring_ref.at[s + 2, 1], hop_send.at[s], recv.at[s + 2, 1], "cp", left)

    def new_copy(source, send, got, where, own=False):
        src = kvn if own else ringn_ref.at[source]
        return remote(src, ringn_ref.at[source], new_send.at[send], new_recv.at[got], "cp", where)

    new_right = new_copy(me, 0, 0, right, own=True)
    new_left = new_copy(me, 1, 1, left, own=True)
    new_pair = new_copy(me, 2, 3, pair, own=True)
    new_hop = new_copy(left, 3, 2, right)
    new_left_pair = new_copy(left, 4, 4, pair)
    new_right_pair = new_copy(right, 5, 5, pair)
    new_far_pair = new_copy(far, 6, 6, pair)

    def pass_on(s):
        for side in range(2):
            from_side(s, side).wait_recv()
            to_pair(s, side).start()

    def cache_in(i):
        here = pl.ds(i * half, half)
        return (pltpu.make_async_copy(kc_ref.at[here], k_buf.at[i, pl.ds(0, half)], in_sem.at[0, i]),
                pltpu.make_async_copy(vc_ref.at[here], v_buf.at[i, pl.ds(0, half)], in_sem.at[1, i]))

    x_in = pltpu.make_async_copy(x_ref, x_buf, in_sem.at[2, 0])

    def res_in(p):
        here = pl.ds(pl.multiple_of(p * PHASE_TOKENS + rank * rows, rows), rows)
        return pltpu.make_async_copy(x_ref.at[here], res_buf.at[p], in_sem.at[2 + p, 1])

    def w_in(j, slot):
        cols = pl.ds(pl.multiple_of(j * COLS, COLS), COLS)
        here = pl.ds(pl.multiple_of(slot * width, width), width)
        return pltpu.make_async_copy(wq_ref.at[:, cols], w_buf.at[here], w_sem.at[slot])

    def wo_at(slot):
        return pl.ds(pl.multiple_of(slot * out_depth, out_depth), out_depth)

    def wo_in(k):
        slot = lax.rem(k, OUT_SLOTS)
        cols = pl.ds(pl.multiple_of(k * COLS, COLS), COLS)
        return pltpu.make_async_copy(wo_ref.at[:, cols], w_buf.at[wo_at(slot)], w_sem.at[slot])

    for i in range(2):
        for copy in cache_in(i):
            copy.start()
    x_in.start()
    w_in(0, 0).start()
    w_in(1, 1).start()
    for p in range(phases):
        res_in(p).start()

    barrier = pltpu.get_barrier_semaphore()
    for other in (pair, right, left):
        pl.semaphore_signal(barrier, inc=1, device_id={"cp": other}, device_id_type=MESH)
    for d in range(1, ranks):
        pl.semaphore_signal(barrier, inc=1, device_id={"tp": lax.rem(rank + d, ranks)}, device_id_type=MESH)

    pair_rows = groups * LANES
    wide = lax.broadcasted_iota(jnp.int32, (pair_rows, pair_rows), 0)
    tall = lax.broadcasted_iota(jnp.int32, (pair_rows, pair_rows), 1)
    pick = (wide // groups + (wide % groups) * LANES == tall).astype(BF16)
    pick_t = (tall // groups + (tall % groups) * LANES == wide).astype(BF16)
    blocks = part // LANES

    def stage_out(c):
        return pltpu.make_async_copy(stage.at[c], ring_ref.at[0, c], out_sem.at[c])

    for c in range(CHUNKS):
        if c % (CHUNKS // 2) == 0:
            for copy in cache_in(c // (CHUNKS // 2)):
                copy.wait()

        def relayout(i, _):
            i_half = c // (CHUNKS // 2)
            src = pl.ds(pl.multiple_of((c % (CHUNKS // 2)) * part * groups + i * pair_rows, pair_rows), pair_rows)
            here = pl.ds(pl.multiple_of(i * LANES, LANES), LANES)
            keys = dot(pick_t, k_buf[i_half, src, :]).astype(BF16)
            vals = dot(v_buf[i_half, src, :], pick, (((0,), (0,)), ((), ()))).astype(BF16)
            for g in range(groups):
                stage[c, g, 0, here, :] = keys[g * LANES:(g + 1) * LANES, :]
                stage[c, g, 1, here, :] = vals[:, g * LANES:(g + 1) * LANES]
            return 0

        lax.fori_loop(0, blocks, relayout, 0, unroll=4)
        stage_out(c).start()
        if c == 0:
            pl.semaphore_wait(barrier, 3 + ranks - 1)
        own_right(c).start()
        own_left(c).start()
        own_pair(c).start()

    x_in.wait()
    gain = g_ref[...].astype(F32)

    def norm(i, _):
        here = pl.ds(pl.multiple_of(i * 32, 32), 32)
        x = x_buf[here, :].astype(F32)
        inv_rms = lax.rsqrt(jnp.mean(x * x, axis=-1, keepdims=True) + EPS)
        hid_ref[here, :] = (x * inv_rms * gain).astype(BF16)
        return 0

    lax.fori_loop(0, tok // 32, norm, 0)
    lane = lax.broadcasted_iota(jnp.int32, (tok, LANES), 1)
    rope_lanes = table_ref.shape[0]
    table = jnp.concatenate([table_ref[...].T, jnp.zeros((tok, LANES - rope_lanes), F32)], axis=1)
    at = jnp.where(lane < rope_lanes, lane // 2, 0)
    sin = jnp.take_along_axis(table, at + rope_lanes // 2, axis=1)
    cos_ref[...] = jnp.take_along_axis(table, at, axis=1)
    sin_ref[...] = jnp.where(lane % 2 == 0, -sin, sin)

    def rotate(head):
        swapped = jnp.where(lane % 2 == 0, pltpu.roll(head, LANES - 1, 1), pltpu.roll(head, 1, 1))
        turned = head * cos_ref[...] + swapped * sin_ref[...]
        return jnp.where(lane < rope_lanes, turned, head)

    def queries(j, i):
        head = j * heads_per_block + i
        g, h = head // (heads + 2), lax.rem(head, heads + 2)
        turned = rotate(a_buf[j, :, i * LANES:(i + 1) * LANES]).T.astype(BF16)
        for p in range(phases):
            tile = jnp.where(h < heads, g * per_group + p * tiles + h // heads_per_tile, spare)
            at = pl.multiple_of(lax.rem(h, heads_per_tile) * PHASE_TOKENS, PHASE_TOKENS)
            qt_ref[tile, :, pl.ds(at, PHASE_TOKENS)] = turned[:, p * PHASE_TOKENS:(p + 1) * PHASE_TOKENS]

    def project(j, _):
        slot = lax.rem(j, 2)
        w_in(j, slot).wait()
        here = pl.ds(pl.multiple_of(slot * width, width), width)
        cols = pl.ds(pl.multiple_of(j * COLS, COLS), COLS)
        before = jnp.maximum(j - 1, 0)
        for i in range(heads_per_block):
            queries(before, i)
        a_buf[j] = dot(hid_ref[...], w_buf[here, :]) + b_ref[:, cols].astype(F32)

        @pl.when(j + 2 < w_blocks)
        def _():
            w_in(j + 2, slot).start()
        return 0

    a_buf[0] = jnp.zeros(a_buf.shape[1:], F32)
    lax.fori_loop(0, w_blocks, project, 0)
    for i in range(heads_per_block):
        queries(w_blocks - 1, i)

    kn_out = pltpu.make_async_copy(kn_buf, kn_ref, out_sem.at[CHUNKS])
    vn_out = pltpu.make_async_copy(vn_buf, vn_ref, out_sem.at[CHUNKS + 1])
    kvn_out = pltpu.make_async_copy(kvn, ringn_ref.at[me], out_sem.at[CHUNKS + 2])
    for g in range(groups):
        at = (g * (heads + 2) + heads) * LANES
        keys = rotate(a_buf[at // COLS, :, at % COLS:at % COLS + LANES]).astype(BF16)
        at += LANES
        vals = a_buf[at // COLS, :, at % COLS:at % COLS + LANES]
        kn_buf[:, g * LANES:(g + 1) * LANES] = keys
        vn_buf[:, g * LANES:(g + 1) * LANES] = vals.astype(BF16)
        kvn[g, 0] = keys
        for i in range(tok // LANES):
            here = slice(i * LANES, (i + 1) * LANES)
            kvn[g, 1, here, :] = vals[here, :].T.astype(BF16)
    for c in range(CHUNKS):
        stage_out(c).wait()

    def fetch(s, g, act):
        for c in range(CHUNKS):
            here = pl.ds(c * part, part)
            for kind, buf in ((0, k_buf), (1, v_buf)):
                getattr(pltpu.make_async_copy(ring_ref.at[s, c, g, kind], buf.at[g, here], fetch_sem.at[g, kind, c]), act)()

    def fetch_new(act):
        for g in range(groups):
            for j in range(n):
                here = pl.ds(g * span_new + j * tok, tok)
                for kind, buf in ((0, k_buf), (1, v_buf)):
                    getattr(pltpu.make_async_copy(ringn_ref.at[j, g, kind], buf.at[0, here], newest_sem.at[kind, g, j]), act)()

    fetch(0, 0, "start")
    kn_out.start()
    vn_out.start()
    kvn_out.start()

    row = lax.broadcasted_iota(jnp.int32, (tok, NC), 0)
    col = lax.rem(lax.broadcasted_iota(jnp.int32, (tok, NC), 1), PHASE_TOKENS)
    bias_ref[0] = jnp.zeros((tok, NC), F32)
    for p in range(phases):
        bias_ref[1 + p] = jnp.where(row <= col + p * PHASE_TOKENS, 0.0, MASK_VALUE)
    bias_ref[1 + phases] = jnp.full((tok, NC), MASK_VALUE, F32)

    m_ref[...] = jnp.full(m_ref.shape, MASK_VALUE, F32)
    l_ref[...] = jnp.zeros(l_ref.shape, F32)
    acc_ref[...] = jnp.zeros(acc_ref.shape, F32)
    s_ref[...] = jnp.zeros(s_ref.shape, F32)
    p_ref[...] = jnp.zeros(p_ref.shape, BF16)
    mc_ref[...] = jnp.zeros(mc_ref.shape, F32)
    al_ref[...] = jnp.ones(al_ref.shape, F32)
    kvn_out.wait()
    for copy in (new_right, new_left, new_pair):
        copy.start()

    def step(a=None, b=None, c=None):
        alpha_b, alpha_c = al_ref[0], al_ref[1]
        shift = mc_ref[...]
        run = {"max": None, "sum": None, "out": None}

        def scores(i):
            keys = k_buf[a["slot"], pl.ds(a["base"] + i * SUB, SUB), :]
            s = dot(keys, qt_ref[a["tile"]])
            if a["new"]:
                edge = 1 + lax.rem(a["tile"], per_group) // tiles
                which = jnp.where(i < me, 0, jnp.where(i == me, edge, 1 + phases))
                s = s + bias_ref[which]
            s_ref[i * SUB:(i + 1) * SUB, :] = s
            top = jnp.max(s.reshape(SUB // 8, 8, NC), axis=0)
            run["max"] = top if run["max"] is None else jnp.maximum(run["max"], top)

        def weights(i):
            s = s_ref[i * SUB:(i + 1) * SUB, :]
            e = jnp.exp2((s * scale).reshape(SUB // 8, 8, NC) - shift[None])
            part_sum = jnp.sum(e, axis=0)
            run["sum"] = part_sum if run["sum"] is None else run["sum"] + part_sum
            p_ref[i * SUB:(i + 1) * SUB, :] = e.reshape(SUB, NC).astype(BF16)

        def values(i):
            at = c["base"] + i * SUB
            block = jnp.concatenate([v_buf[c["slot"], pl.ds(at + h * LANES, LANES), :] for h in range(SUB // LANES)], axis=1)
            out = dot(block, p_ref[i * SUB:(i + 1) * SUB, :])
            run["out"] = out if run["out"] is None else run["out"] + out

        stages = ((c, values), (b, weights), (a, scores))
        for i in range(max(spec["keys"] for spec, _ in stages if spec is not None) // SUB):
            for spec, stage_fn in stages:
                if spec is not None and i < spec["keys"] // SUB:
                    stage_fn(i)
        if c is not None:
            acc_ref[c["tile"]] = acc_ref[c["tile"]] * alpha_c + run["out"]
        if b is not None:
            l_ref[b["tile"]] = l_ref[b["tile"]] * alpha_b + run["sum"]
            al_ref[1] = alpha_b
        if a is not None:
            old = m_ref[a["tile"]]
            new = jnp.maximum(old, jnp.max(run["max"], axis=0, keepdims=True))
            m_ref[a["tile"]] = new
            mc_ref[...] = jnp.broadcast_to(new * scale, mc_ref.shape)
            al_ref[0] = jnp.exp2((old - new) * scale)

    def main(tile, slot):
        return {"tile": tile, "slot": slot, "base": 0, "keys": span, "new": False}

    def run_unit(g, first, tile_count, carry, fetch_next):
        fetch(0, g, "wait")

        def one_tile(t, carry):
            pl.when(t == tile_count - 1)(fetch_next)
            last, last_slot, older, older_slot = carry
            tile = g * per_group + first + t
            step(main(tile, g), main(last, last_slot), main(older, older_slot))
            return tile, jnp.int32(g), last, last_slot

        return lax.fori_loop(0, tile_count, one_tile, carry)

    start = tuple(jnp.int32(v) for v in (spare, 0, spare, 0))

    def one_set(s, carry):
        nxt = s + 1
        carry = run_unit(0, 0, per_group, carry, lambda: fetch(s, 1, "start"))
        pl.when(s >= 1)(lambda: pass_on(nxt))
        pl.when((s >= 1) & (s <= 2))(lambda: hop_right(nxt).start())
        pl.when((s >= 3) & (s <= 4))(lambda: hop_left(nxt).start())

        def fetch_next():
            @pl.when(s == 0)
            def _():
                for c in range(CHUNKS):
                    own_pair(c).wait_recv()

            @pl.when(s >= 1)
            def _():
                for side in range(2):
                    to_pair(nxt, side).wait_recv()
            fetch(nxt, 0, "start")

        return run_unit(1, 0, per_group, carry, fetch_next)

    carry = lax.fori_loop(0, n - 2, one_set, start)
    kn_out.wait()
    vn_out.wait()

    def part_copy(p, k, d):
        to = lax.rem(rank + d, ranks)
        src = send_buf.at[k, pl.ds(pl.multiple_of(to * rows, rows), rows)]
        return remote(src, got_buf.at[p, k, d - 1], part_send.at[p, k, d - 1], part_recv.at[p, k, d - 1], "tp", to)

    def y_rows(p):
        return pl.ds(pl.multiple_of(p * PHASE_TOKENS + rank * rows, rows), rows)

    def y_copy(p, k, d):
        cols = pl.ds(pl.multiple_of(k * COLS, COLS), COLS)
        to = lax.rem(rank + d, ranks)
        return remote(y_buf.at[p, k], y_ref.at[y_rows(p), cols], y_send.at[p, k, d - 1], y_recv.at[p, k, d - 1], "tp", to)

    def y_own(p, k):
        cols = pl.ds(pl.multiple_of(k * COLS, COLS), COLS)
        return pltpu.make_async_copy(y_buf.at[p, k], y_ref.at[y_rows(p), cols], y_sem.at[p, k])

    def project_out(p):
        def piece(k, _):
            @pl.when(k < pieces)
            def _():
                wo_in(k).wait()
                out = dot(o_buf[...], w_buf[wo_at(lax.rem(k, OUT_SLOTS)), :])
                full_buf[...] = out
                send_buf[k] = out.astype(BF16)
                mine_buf[k] = full_buf[pl.ds(pl.multiple_of(rank * rows, rows), rows), :]
                pl.when(k + OUT_SLOTS < pieces)(lambda: wo_in(k + OUT_SLOTS).start())

            @pl.when(k >= 1)
            def _():
                for d in range(1, ranks):
                    part_copy(p, k - 1, d).start()
            return 0

        lax.fori_loop(0, pieces + 1, piece, 0)

    def reduce_out(p, lo, hi):
        def piece(k, _):
            @pl.when(k < hi)
            def _():
                for d in range(1, ranks):
                    part_copy(p, k, d).wait_recv()
                total = mine_buf[k]
                for d in range(1, ranks):
                    total = total + got_buf[p, k, d - 1].astype(F32)
                cols = pl.ds(pl.multiple_of(k * COLS, COLS), COLS)
                y_buf[p, k] = (res_buf[p, :, cols].astype(F32) + total).astype(BF16)

            @pl.when(k > lo)
            def _():
                y_own(p, k - 1).start()
                for d in range(1, ranks):
                    y_copy(p, k - 1, d).start()
            return 0

        lax.fori_loop(lo, hi + 1, piece, 0)

    def finish(p, g):
        def tile(h, _):
            t = g * per_group + p * tiles + h
            total = jnp.sum(l_ref[t], axis=0, keepdims=True)
            out = (acc_ref[t] / total).T.astype(BF16)
            for i in range(heads_per_tile):
                at = pl.multiple_of((g * heads + h * heads_per_tile + i) * LANES, LANES)
                o_buf[:, pl.ds(at, LANES)] = out[i * PHASE_TOKENS:(i + 1) * PHASE_TOKENS, :]
            return 0

        lax.fori_loop(0, tiles, tile, 0)

    for p in range(phases):
        res_in(p).wait()

    def one_phase(p, carry):
        first = p * tiles

        def late_set(s, carry):
            carry = run_unit(0, first, tiles, carry, lambda: fetch(s, 1, "start"))

            @pl.when((p == 0) & (s == n - 2))
            def _():
                pass_on(n - 1)
                new_copy(left, 0, 0, right).wait_recv()
                new_hop.start()
                new_left_pair.start()
                new_copy(right, 0, 1, left).wait_recv()
                new_right_pair.start()

            @pl.when((p == 0) & (s == n - 1))
            def _():
                new_copy(far, 0, 2, right).wait_recv()
                new_far_pair.start()

            @pl.when((p > 0) & (s == n - 1))
            def _():
                reduce_out(p - 1, 0, pieces // 2)

            def fetch_next():
                @pl.when(s == n - 2)
                def _():
                    @pl.when(p == 0)
                    def _():
                        for side in range(2):
                            to_pair(n - 1, side).wait_recv()
                    fetch(n - 1, 0, "start")

            return run_unit(1, first, tiles, carry, fetch_next)

        carry = lax.fori_loop(n - 2, n, late_set, carry)
        last, last_slot, older, older_slot = carry

        @pl.when(p == 0)
        def _():
            for got in (3, 4, 5, 6):
                new_copy(pair, 0, got, pair).wait_recv()

        @pl.when(p > 0)
        def _():
            reduce_out(p - 1, pieces // 2, pieces)
        fetch_new("start")
        for k in range(OUT_SLOTS):
            wo_in(k).start()
        fetch_new("wait")

        def recent(i):
            g = i // tiles
            return {"tile": g * per_group + first + lax.rem(i, tiles), "slot": 0, "base": pl.multiple_of(g * span_new, span_new), "keys": span_new, "new": True}

        step(recent(0), main(last, last_slot), main(older, older_slot))
        step(recent(1), recent(0), main(last, last_slot))

        def new_tile(i, _):
            step(recent(i), recent(i - 1), recent(i - 2))
            return 0

        end = groups * tiles
        lax.fori_loop(2, end, new_tile, 0)
        step(None, recent(end - 1), recent(end - 2))
        step(None, None, recent(end - 1))

        @pl.when(p < phases - 1)
        def _():
            fetch(n - 2, 0, "start")
        for g in range(groups):
            finish(p, g)

        @pl.when(p > 0)
        def _():
            def sent(k, _):
                for d in range(1, ranks):
                    part_copy(p - 1, k, d).wait_send()
                return 0
            lax.fori_loop(0, pieces, sent, 0)
        project_out(p)
        return start

    lax.fori_loop(0, phases, one_phase, carry)
    reduce_out(phases - 1, 0, pieces)

    for c in range(CHUNKS):
        own_right(c).wait_send()
        own_left(c).wait_send()
        own_pair(c).wait_send()
    for s in range(2, n):
        for side in range(2):
            to_pair(s, side).wait_send()
    for s in (2, 3):
        hop_right(s).wait_send()
    for s in (4, 5):
        hop_left(s).wait_send()
    for copy in (new_right, new_left, new_pair, new_hop, new_left_pair, new_right_pair, new_far_pair):
        copy.wait_send()

    def drain(k, _):
        for d in range(1, ranks):
            part_copy(phases - 1, k, d).wait_send()
        for p in range(phases):
            y_own(p, k).wait()
            for d in range(1, ranks):
                y_copy(p, k, d).wait_send()
                y_copy(p, k, d).wait_recv()
        return 0

    lax.fori_loop(0, pieces, drain, 0)


def local_step(n, ranks, x, k_cache, v_cache, rope_table, norm_gain, w_qkv, b_qkv, w_out):
    positions, groups, head_dim = k_cache.shape
    tok, width = x.shape
    heads = w_qkv.shape[1] // groups // head_dim - 2
    part = positions // CHUNKS
    span, span_new = positions, n * tok
    phases = tok // PHASE_TOKENS
    tiles = heads * PHASE_TOKENS // NC
    count = groups * phases * tiles
    rows_max = max(span, groups * span_new)
    pieces = width // COLS
    w_blocks = w_qkv.shape[1] // COLS
    rows = PHASE_TOKENS // ranks
    depth = w_out.shape[0]
    any_spec = pl.BlockSpec(memory_space=pl.ANY)
    vmem_spec = pl.BlockSpec(memory_space=pltpu.VMEM)
    flat = (positions * groups, head_dim)
    flops = 4 * count * NC * LANES * n * (span + tok)
    y, new_k, new_v, _, _ = pl.pallas_call(
        functools.partial(block_kernel, (n, ranks, groups, heads)),
        in_specs=[any_spec, any_spec, any_spec, vmem_spec, vmem_spec, any_spec, vmem_spec, any_spec],
        out_specs=[any_spec] * 5,
        out_shape=[
            jax.ShapeDtypeStruct((tok, width), BF16),
            jax.ShapeDtypeStruct((tok, groups * head_dim), BF16),
            jax.ShapeDtypeStruct((tok, groups * head_dim), BF16),
            jax.ShapeDtypeStruct((n, CHUNKS, groups, 2, part, head_dim), BF16),
            jax.ShapeDtypeStruct((n, groups, 2, tok, head_dim), BF16),
        ],
        scratch_shapes=[
            pltpu.VMEM((2, rows_max, LANES), BF16),
            pltpu.VMEM((2, rows_max, LANES), BF16),
            pltpu.VMEM((CHUNKS, groups, 2, part, LANES), BF16),
            pltpu.VMEM((groups, 2, tok, LANES), BF16),
            pltpu.VMEM((count + 1, LANES, NC), BF16),
            pltpu.VMEM((tok, width), BF16),
            pltpu.VMEM((tok, width), BF16),
            pltpu.VMEM((max(2 * width, OUT_SLOTS * depth), COLS), BF16),
            pltpu.VMEM((w_blocks, tok, COLS), F32),
            pltpu.VMEM((tok, LANES), F32),
            pltpu.VMEM((tok, LANES), F32),
            pltpu.VMEM((tok, groups * LANES), BF16),
            pltpu.VMEM((tok, groups * LANES), BF16),
            pltpu.VMEM((max(span, span_new), NC), F32),
            pltpu.VMEM((max(span, span_new), NC), BF16),
            pltpu.VMEM((count + 1, LANES, NC), F32),
            pltpu.VMEM((count, 1, NC), F32),
            pltpu.VMEM((count + 1, 8, NC), F32),
            pltpu.VMEM((8, NC), F32),
            pltpu.VMEM((2, 1, NC), F32),
            pltpu.VMEM((2 + phases, tok, NC), F32),
            pltpu.VMEM((PHASE_TOKENS, groups * heads * LANES), BF16),
            pltpu.VMEM((phases, rows, width), BF16),
            pltpu.VMEM((PHASE_TOKENS, COLS), F32),
            pltpu.VMEM((pieces, rows, COLS), F32),
            pltpu.VMEM((pieces, PHASE_TOKENS, COLS), BF16),
            pltpu.VMEM((phases, pieces, ranks - 1, rows, COLS), BF16),
            pltpu.VMEM((phases, pieces, rows, COLS), BF16),
            DMA((2 + phases, 2)),
            DMA((max(2, OUT_SLOTS),)),
            DMA((CHUNKS + 3,)),
            DMA((groups, 2, CHUNKS)),
            DMA((2, groups, n)),
            DMA((3, CHUNKS)),
            DMA((n, 2)),
            DMA((n,)),
            DMA((7,)),
            DMA((n, CHUNKS)),
            DMA((7,)),
            DMA((phases, pieces, ranks - 1)),
            DMA((phases, pieces, ranks - 1)),
            DMA((phases, pieces, ranks - 1)),
            DMA((phases, pieces, ranks - 1)),
            DMA((phases, pieces)),
        ],
        cost_estimate=pl.CostEstimate(flops=flops, bytes_accessed=4 * positions * n * groups * head_dim, transcendentals=flops // (4 * LANES)),
        compiler_params=pltpu.CompilerParams(collective_id=0, has_side_effects=True, vmem_limit_bytes=63 << 20),
        name="block",
    )(x, k_cache.reshape(flat), v_cache.reshape(flat), rope_table.T, norm_gain.reshape(1, width), w_qkv, b_qkv.reshape(1, -1), w_out)
    new_shape = (tok,) + k_cache.shape[1:]
    return y, new_k.reshape(new_shape), new_v.reshape(new_shape)


def solution(mesh):
    row_spec = P(("dp", "cp"), None)
    cache_spec = P(("dp", "cp"), "tp", None)
    body = functools.partial(local_step, mesh.shape["cp"], mesh.shape["tp"])
    return jax.shard_map(body, mesh=mesh, in_specs=(row_spec, cache_spec, cache_spec, row_spec, P(None), P(None, "tp"), P("tp"), P("tp", None)), out_specs=(row_spec, cache_spec, cache_spec), check_vma=False)
```

time: 1330 us -> 295 us (0.22)
  matrix products: 676 us -> 0 us
  waiting for transfers between devices: 301 us -> 0 us
  other arithmetic: 297 us -> 0 us
  Pallas kernels: 0 us -> 284 us
  local copies, waits for them, and re-layouts: 33.8 us -> 9.21 us
  between operations: 14 us -> 0.64 us
    dot_general x34 -> x0, matrix products: 676 us -> none  [the longest x8 291 us: attend(): jnp.einsum('tngd,knd->tngk', queries, kp_block, preferred_element_type=jn...]
    reduce_sum x17 -> x0, other arithmetic: 285 us -> none  [the longest x16 283 us: attend(): run_sum = run_sum * rescale + p_pref.sum(axis=-1) + p_recent.sum(axis=-1)]
    pallas_call x0 -> x1, Pallas kernels: none -> 284 us  [local_step(): pl.pallas_call(functools.partial(block_kernel, (n, ranks, groups, heads))...]
    all_gather x4 -> x0, waiting for transfers between devices: 199 us -> none  [the longest x1 84.7 us: local_step(): k_prefix = lax.all_gather(k_cache, 'cp')]
    psum x1 -> x0, waiting for transfers between devices: 101 us -> none  [local_step(): y = (x_f32 + lax.psum(proj_part, 'tp')).astype(jnp.bfloat16)]
  transfers between devices with their start and end apart: 5 -> 0, of which waited for: 5 -> 0; matrix products, arithmetic and copies ran while one was open for 2% -> 0% of each run, Pallas kernels for 0% -> 0%
where the time goes in v2:
time: 295 us; the launch traced here: 294 us
  Pallas kernels  284 us (96%)
  local copies, waits for them, and re-layouts  9.21 us (3%)
    pallas_call x1, Pallas kernels, local_step(): pl.pallas_call(functools.partial(block_kernel, (n, ranks, groups, heads))...  284 us

profile of v2, /device:TPU:97, one launch (start us, length us, event | category | flops | bytes accessed | tf_op | source)
XLA Modules:
  0.0 294.3 jit_solution(18288623404793332212)
XLA Ops:
  0.6 1.3 reshape.27.b_ref
  1.9 1.3 reshape.26.g_ref
  3.3 284.5 %block.1 = (bf16[256,5120]{1,0:T(8,128)(2,1)}, bf16[256,256]{1,0:T(8,128)(2,1)}, bf16[256,256]{1,0:T(8,128)(2,1)}, bf16[8,4,2,2,1024,128]{5,4,3,2,1,0:T(8,128)(2,1)}, bf16[8,2,2,256,128]{4,3,2,1,0:T(8,128)(2,1)}) custom-call(bf16[256,5120]{1,0:T(8,128)(2,1)} %x_ref.1, bf16[8192,128]{1,0:T(8,128)(2,1)} %bitcast.3, bf16[8192,128]{1,0:T(8,128)(2,1)} %bitcast.4, ...), custom_call_target="tpu_custom_call" | custom-call | flops 109521666048 | bytes 33554432 | tf_op jit(solution)/shard_map/block/pallas_call | solution.py:571
  287.7 1.6 reshape.28
  289.3 1.6 reshape.29
  290.9 3.4 %copy.12 = bf16[256,5120]{1,0:T(8,128)(2,1)} copy(bf16[256,5120]{1,0:T(8,128)(2,1)} %get-tuple-element.12) | data formatting | bytes 5242880
